TPU v7x, 256 devices: a whole 4x4x8 slice. The times are simulated.
256 devices in a mesh: py: 16 (over z_lo, y_hi, x), px: 4 (over z_hi), pz: 4 (over y_lo, core).
Axes of the slice: x: 4, y: 4 (y_hi: 2, y_lo: 2; y = y_hi * 2 + y_lo), z: 8 (z_hi: 4, z_lo: 2; z = z_hi * 2 + z_lo), core: 2. Of those that a mesh axis runs over, the one named last changes fastest.
Arguments:
- field_now: float32 [128, 64, 256, 128], P('py', 'px', 'pz'), may hold values from 0.2 to 1.8
- earlier: float32 [128, 64, 256, 128], P('py', 'px', 'pz'), may hold values from 0.2 to 1.8
- speed_square: float32 [128, 64, 256, 128], P('py', 'px', 'pz'), may hold values from 0.05 to 0.3
Outputs:
- column_sum: float32 [128, 64, 256, 128], P('py', 'px', 'pz')
- field_now_end: float32 [128, 64, 256, 128], P('py', 'px', 'pz')
All inputs are finite; a program needn't handle non-finite values.
Results may differ from a plain program's by a relative error of at most 0.00002.
Values sent between devices are 32-bit elements; how exact they have to be, the bound alone decides.
A program may use at most 128 MiB of HBM per device.

v0:
```python
import jax
import jax.numpy as jnp
from jax import lax
from jax.sharding import Mesh
from jax.sharding import PartitionSpec as P

STEPS = 4
PY = ("py_0", "py_1", "py_2")


def padded_2(value, sides, width):
    edges = {}
    for axis, dim in sides:
        peers, length = (lax.axis_size(axis), value.shape[dim])
        up = [(i, (i + 1) % peers) for i in range(peers)]
        last = lax.slice_in_dim(value, length - width, length, axis=dim)
        initial = lax.slice_in_dim(value, 0, width, axis=dim)
        edges[dim] = (
            lax.ppermute(last, axis, up),
            lax.ppermute(initial, axis, [(b, a) for a, b in up]),
        )
    done = []
    for _, dim in sides:
        low, high = edges[dim]
        around = [(width, width) if d in done else (0, 0) for d in range(value.ndim)]
        value = jnp.concatenate([jnp.pad(low, around), value, jnp.pad(high, around)], axis=dim)
        done.append(dim)
    return value


def neutral_like(value, identity):
    return jnp.broadcast_to(jnp.asarray(identity, value.dtype), value.shape)


def prefix_by_axis(value, axes, combine, identity):
    before = start = neutral_like(value, identity)
    so_far = value
    for axis in reversed(axes):
        peers, mine = (lax.axis_size(axis), lax.axis_index(axis))
        pieces = lax.all_gather(so_far, axis)
        inside, so_far = (start, start)
        for k in range(peers):
            passed = k < mine
            so_far = combine(so_far, pieces[k])
            inside = jnp.where(passed, so_far, inside)
        before = combine(inside, before)
    return before


def without_rim(values, dims):
    for dim in dims:
        values = lax.slice_in_dim(values, 1, values.shape[dim] - 1, axis=dim)
    return values


def shifted_cells(values, dim, start, dims):
    others = [other for other in dims if other != dim]
    values = without_rim(values, others)
    return lax.slice_in_dim(values, start, start + values.shape[dim] - 2, axis=dim)


def march_step(padded, before, speed_square):
    middle = without_rim(padded, (0, 1, 2))
    lower = [shifted_cells(padded, dim, 0, (0, 1, 2)) for dim in (0, 1, 2)]
    upper = [shifted_cells(padded, dim, 2, (0, 1, 2)) for dim in (0, 1, 2)]
    spread = lower[0] + upper[0] + lower[1] + upper[1] + lower[2] + upper[2] - 6.0 * middle
    return 2.0 * middle - before + speed_square * spread


def local(field_now, earlier, speed_square):
    for step in range(STEPS):
        padded = padded_2(field_now, ((PY, 0), ("px", 1), ("pz", 2)), 1)
        later = march_step(padded, earlier, speed_square)
        earlier, field_now = (field_now, later)
    here = jnp.cumsum(field_now, axis=0)
    total = lax.slice_in_dim(here, here.shape[0] - 1, here.shape[0], axis=0)

    def add_pair(earlier_total, later_total):
        return earlier_total + later_total

    below = prefix_by_axis(total, PY, add_pair, jnp.zeros_like(total))
    column_sum = (here + below) / (field_now.shape[0] * lax.axis_size(PY))
    return (column_sum, field_now)


def solution(mesh):
    torus = Mesh(
        mesh.devices.reshape(2, 2, 4, mesh.shape["px"], mesh.shape["pz"]),
        ("py_0", "py_1", "py_2", "px", "pz"),
    )
    placed = (P(PY, "px", "pz", None), P(PY, "px", "pz", None), P(PY, "px", "pz", None))
    return jax.shard_map(
        local,
        mesh=torus,
        in_specs=placed,
        out_specs=(P(PY, "px", "pz", None), P(PY, "px", "pz", None)),
        check_vma=False,
    )
```

profile of v0, /device:TPU:8, one launch (start us, length us, event | category | flops | bytes accessed | tf_op | source)
XLA Modules:
  0.0 288.4 jit_solution(4413920224108575795)
XLA Ops:
  7.2 0.0 all-gather.9.cloned.1.call-start
  7.2 1.4 fusion.56
  8.7 1.6 collective-permute-start
  10.2 1.1 fusion.55
  11.3 3.3 %collective-permute-start.2 = (f32[8,1,64,128]{3,2,1,0:T(8,128)S(1)}, f32[8,1,64,128]{3,2,1,0:T(8,128)S(1)}, u32[]{:S(2)}, u32[]{:S(2)}) collective-permute-start(f32[8,1,64,128]{3,2,1,0:T(8,128)S(1)} %get-tuple-element.22), channel_id=1, source_target_pairs={{0,4},{4,8},{8,12},{12,0},{1,5},{5,9},{9,13},{13,1},{2,6},{6,10},{... | collective-permute-start | bytes 786440 | tf_op jit(solution)/shard_map/ppermute | solution.py:19
  14.7 3.1 %collective-permute-start.3 = (f32[8,1,64,128]{3,2,1,0:T(8,128)S(1)}, f32[8,1,64,128]{3,2,1,0:T(8,128)S(1)}, u32[]{:S(2)}, u32[]{:S(2)}) collective-permute-start(f32[8,1,64,128]{3,2,1,0:T(8,128)S(1)} %get-tuple-element.23), channel_id=1, source_target_pairs={{4,0},{8,4},{12,8},{0,12},{5,1},{9,5},{13,9},{1,13},{6,2},{10,6},{... | collective-permute-start | bytes 786440 | tf_op jit(solution)/shard_map/ppermute | solution.py:20
  17.8 5.0 %collective-permute-start.1 = (f32[1,16,64,128]{3,2,1,0:T(8,128)S(1)}, f32[1,16,64,128]{3,2,1,0:T(8,128)S(1)}, u32[]{:S(2)}, u32[]{:S(2)}) collective-permute-start(f32[1,16,64,128]{3,2,1,0:T(8,128)S(1)} %get-tuple-element.24), channel_id=1, source_target_pairs={{16,0},{32,16},{48,32},{64,48},{80,64},{96,80},{112,96},{128,112},... | collective-permute-start | bytes 1572872 | tf_op jit(solution)/shard_map/ppermute | solution.py:20
  22.8 1.3 fusion.54
  24.1 0.1 collective-permute-start.4
  24.2 1.8 collective-permute-done.2
  26.1 4.4 %collective-permute-done.3 = f32[8,1,64,128]{3,2,1,0:T(8,128)S(1)} collective-permute-done((f32[8,1,64,128]{3,2,1,0:T(8,128)S(1)}, f32[8,1,64,128]{3,2,1,0:T(8,128)S(1)}, u32[]{:S(2)}, u32[]{:S(2)}) %collective-permute-start.3) | collective-permute-done | bytes 262176 | tf_op jit(solution)/shard_map/ppermute | solution.py:20
  30.5 0.8 pad.51
  31.2 2.4 collective-permute-done
  33.7 0.9 constant_dynamic-update-slice_fusion.2
  34.5 2.7 constant_dynamic-update-slice_fusion.1
  37.2 0.9 constant_dynamic-update-slice_fusion
  38.1 0.3 copy-done
  38.3 14.0 %fusion.34 = f32[8,16,64,128]{3,2,1,0:T(8,128)} fusion(f32[8,16,64,128]{3,2,1,0:T(8,128)S(1)} %copy-done, f32[8,16,1,128]{3,2,1,0:T(1,128)S(1)} %collective-permute-done.5, f32[10,1,64,128]{3,2,1,0:T(8,128)} %pad.51, f32[10,16,64,128]{3,2,1,0:T(8,128)} %constant_dynamic-update-slice_fusion, f32[10,1,64,128]{3,2,1,0:T(8,128)S(1)} %pad.50, ...), kind=kLoop, calls=%fused_computation.89 | loop fusion | flops 28311552 | bytes 23855104 | tf_op jit(solution)/shard_map/add | solution.py:67
  52.3 1.4 fusion.52
  53.8 0.1 collective-permute-start.6
  53.9 8.6 %collective-permute-start.7 = (f32[1,16,64,128]{3,2,1,0:T(8,128)S(1)}, f32[1,16,64,128]{3,2,1,0:T(8,128)S(1)}, u32[]{:S(2)}, u32[]{:S(2)}) collective-permute-start(f32[1,16,64,128]{3,2,1,0:T(8,128)S(1)} %get-tuple-element.17), channel_id=1, source_target_pairs={{16,0},{32,16},{48,32},{64,48},{80,64},{96,80},{112,96},{128,112},... | collective-permute-start | bytes 1572872 | tf_op jit(solution)/shard_map/ppermute | solution.py:20
  62.5 1.1 fusion.53
  63.5 4.6 %collective-permute-start.8 = (f32[8,1,64,128]{3,2,1,0:T(8,128)S(1)}, f32[8,1,64,128]{3,2,1,0:T(8,128)S(1)}, u32[]{:S(2)}, u32[]{:S(2)}) collective-permute-start(f32[8,1,64,128]{3,2,1,0:T(8,128)S(1)} %get-tuple-element.18), channel_id=1, source_target_pairs={{0,4},{4,8},{8,12},{12,0},{1,5},{5,9},{9,13},{13,1},{2,6},{6,10},{... | collective-permute-start | bytes 786440 | tf_op jit(solution)/shard_map/ppermute | solution.py:19
  68.1 1.3 fusion.51
  69.4 0.3 collective-permute-start.10
  69.7 17.6 %collective-permute-done.8 = f32[8,1,64,128]{3,2,1,0:T(8,128)S(1)} collective-permute-done((f32[8,1,64,128]{3,2,1,0:T(8,128)S(1)}, f32[8,1,64,128]{3,2,1,0:T(8,128)S(1)}, u32[]{:S(2)}, u32[]{:S(2)}) %collective-permute-start.8) | collective-permute-done | bytes 262176 | tf_op jit(solution)/shard_map/ppermute | solution.py:19
  87.4 1.8 collective-permute-done.11
  89.2 8.0 %fusion.24 = f32[8,16,64,128]{3,2,1,0:T(8,128)S(1)} fusion(f32[8,16,64,128]{3,2,1,0:T(8,128)S(1)} %copy-done, f32[8,16,1,128]{3,2,1,0:T(1,128)S(1)} %collective-permute-done.11, f32[10,1,64,128]{3,2,1,0:T(8,128)S(1)} %pad.55, f32[10,1,64,128]{3,2,1,0:T(8,128)S(1)} %pad.54, f32[1,16,64,128]{3,2,1,0:T(8,128)S(1)} %collective-permute-done.7, ...), kind=kLoop, calls=%fused_computation.61 | loop fusion | flops 36700160 | bytes 18612224 | tf_op jit(solution)/shard_map/add | solution.py:67
  97.2 0.1 fusion.49
  97.3 0.1 collective-permute-start.12
  97.4 6.5 %collective-permute-start.13 = (f32[1,16,64,128]{3,2,1,0:T(8,128)S(1)}, f32[1,16,64,128]{3,2,1,0:T(8,128)S(1)}, u32[]{:S(2)}, u32[]{:S(2)}) collective-permute-start(f32[1,16,64,128]{3,2,1,0:T(8,128)S(1)} %get-tuple-element.11), channel_id=1, source_target_pairs={{16,0},{32,16},{48,32},{64,48},{80,64},{96,80},{112,96},{128,112},... | collective-permute-start | bytes 1572872 | tf_op jit(solution)/shard_map/ppermute | solution.py:20
  104.0 1.3 collective-permute-start.14
  105.3 2.9 %collective-permute-start.15 = (f32[8,1,64,128]{3,2,1,0:T(8,128)S(1)}, f32[8,1,64,128]{3,2,1,0:T(8,128)S(1)}, u32[]{:S(2)}, u32[]{:S(2)}) collective-permute-start(f32[8,1,64,128]{3,2,1,0:T(8,128)S(1)} %get-tuple-element.13), channel_id=1, source_target_pairs={{4,0},{8,4},{12,8},{0,12},{5,1},{9,5},{13,9},{1,13},{6,2},{10,6},{... | collective-permute-start | bytes 786440 | tf_op jit(solution)/shard_map/ppermute | solution.py:20
  108.2 0.1 fusion.48
  108.3 0.1 collective-permute-start.16
  108.4 22.0 %collective-permute-done.14 = f32[8,1,64,128]{3,2,1,0:T(8,128)S(1)} collective-permute-done((f32[8,1,64,128]{3,2,1,0:T(8,128)S(1)}, f32[8,1,64,128]{3,2,1,0:T(8,128)S(1)}, u32[]{:S(2)}, u32[]{:S(2)}) %collective-permute-start.14) | collective-permute-done | bytes 262176 | tf_op jit(solution)/shard_map/ppermute | solution.py:19
  130.4 0.5 collective-permute-start.17
  131.0 1.8 collective-permute-done.17
  132.9 8.0 %fusion.14 = f32[8,16,64,128]{3,2,1,0:T(8,128)S(1)} fusion(f32[8,16,64,128]{3,2,1,0:T(8,128)S(1)} %copy-done, f32[8,16,1,128]{3,2,1,0:T(1,128)S(1)} %collective-permute-done.17, f32[10,1,64,128]{3,2,1,0:T(8,128)S(1)} %pad.59, f32[10,1,64,128]{3,2,1,0:T(8,128)S(1)} %pad.58, f32[1,16,64,128]{3,2,1,0:T(8,128)S(1)} %collective-permute-done.13, ...), kind=kLoop, calls=%fused_computation.33 | loop fusion | flops 36700160 | bytes 18612224 | tf_op jit(solution)/shard_map/add | solution.py:67
  140.9 0.1 fusion.46
  141.0 0.1 collective-permute-start.18
  141.1 6.5 %collective-permute-start.19 = (f32[1,16,64,128]{3,2,1,0:T(8,128)S(1)}, f32[1,16,64,128]{3,2,1,0:T(8,128)S(1)}, u32[]{:S(2)}, u32[]{:S(2)}) collective-permute-start(f32[1,16,64,128]{3,2,1,0:T(8,128)S(1)} %get-tuple-element.5), channel_id=1, source_target_pairs={{16,0},{32,16},{48,32},{64,48},{80,64},{96,80},{112,96},{128,112},... | collective-permute-start | bytes 1572872 | tf_op jit(solution)/shard_map/ppermute | solution.py:20
  147.7 0.4 collective-permute-start.20
  148.1 3.8 %collective-permute-start.21 = (f32[8,1,64,128]{3,2,1,0:T(8,128)S(1)}, f32[8,1,64,128]{3,2,1,0:T(8,128)S(1)}, u32[]{:S(2)}, u32[]{:S(2)}) collective-permute-start(f32[8,1,64,128]{3,2,1,0:T(8,128)S(1)} %get-tuple-element.7), channel_id=1, source_target_pairs={{4,0},{8,4},{12,8},{0,12},{5,1},{9,5},{13,9},{1,13},{6,2},{10,6},{... | collective-permute-start | bytes 786440 | tf_op jit(solution)/shard_map/ppermute | solution.py:20
  151.9 0.1 fusion.45
  152.0 3.9 %collective-permute-start.22 = (f32[8,16,1,128]{3,2,1,0:T(1,128)S(1)}, f32[8,16,1,128]{3,2,1,0:T(1,128)S(1)}, u32[]{:S(2)}, u32[]{:S(2)}) collective-permute-start(f32[8,16,1,128]{3,2,1,0:T(1,128)S(1)} %get-tuple-element.2), channel_id=1, source_target_pairs={{0,1},{1,2},{2,3},{3,0},{4,5},{5,6},{6,7},{7,4},{8,9},{9,10},{10,1... | collective-permute-start | bytes 196616 | tf_op jit(solution)/shard_map/ppermute | solution.py:19
  155.9 11.2 %collective-permute-done.20 = f32[8,1,64,128]{3,2,1,0:T(8,128)S(1)} collective-permute-done((f32[8,1,64,128]{3,2,1,0:T(8,128)S(1)}, f32[8,1,64,128]{3,2,1,0:T(8,128)S(1)}, u32[]{:S(2)}, u32[]{:S(2)}) %collective-permute-start.20) | collective-permute-done | bytes 262176 | tf_op jit(solution)/shard_map/ppermute | solution.py:19
  167.1 1.9 collective-permute-start.23
  169.1 1.8 collective-permute-done.23
  170.9 8.0 %fusion.4 = f32[8,16,64,128]{3,2,1,0:T(8,128)S(1)} fusion(f32[8,16,64,128]{3,2,1,0:T(8,128)S(1)} %copy-done, f32[8,16,1,128]{3,2,1,0:T(1,128)S(1)} %collective-permute-done.23, f32[10,1,64,128]{3,2,1,0:T(8,128)S(1)} %pad.63, f32[10,1,64,128]{3,2,1,0:T(8,128)S(1)} %pad.62, f32[1,16,64,128]{3,2,1,0:T(8,128)S(1)} %collective-permute-done.19, ...), kind=kLoop, calls=%fused_computation.5 | loop fusion | flops 36700160 | bytes 18612224 | tf_op jit(solution)/shard_map/add | solution.py:67
  179.0 5.4 %fusion.57 = f32[8,16,64,128]{3,2,1,0:T(8,128)S(1)} fusion(f32[8,16,64,128]{3,2,1,0:T(8,128)S(1)} %fusion.4), kind=kOutput, calls=%fused_computation.133 | output fusion | flops 7340032 | bytes 8388608 | tf_op jit(solution)/shard_map/jit(cumsum)/reduce_window_sum | solution.py:75
  184.4 2.0 copy-done.3
  186.4 0.8 slice.406
  187.3 0.0 all-gather.9.cloned.1.call-update
  187.3 0.0 all-gather.5.cloned.1.call-start
  187.4 29.8 %all-gather.9.cloned.1.call-done = f32[4,16,64,128]{3,2,1,0:T(8,128)} async-done(((f32[1,16,64,128]{3,2,1,0:T(8,128)}), f32[4,16,64,128]{3,2,1,0:T(8,128)}) %all-gather.9.cloned.1.call-update) | async-done | bytes 2097168 | tf_op jit(solution)/shard_map/all_gather | solution.py:40
  217.2 2.6 fusion.43
  219.9 0.0 all-gather.7.cloned.1.call-start
  219.9 27.2 %all-gather.5.cloned.1.call-done = f32[2,1,16,64,128]{4,3,2,1,0:T(8,128)} async-done(((f32[1,1,16,64,128]{4,3,2,1,0:T(8,128)}), f32[2,1,16,64,128]{4,3,2,1,0:T(8,128)}) %all-gather.5.cloned.1.call-update) | async-done | bytes 1048592 | tf_op jit(solution)/shard_map/all_gather | solution.py:40
  247.1 2.1 slice_add_fusion.1
  249.2 26.9 %all-gather.7.cloned.1.call-done = f32[2,1,16,64,128]{4,3,2,1,0:T(8,128)} async-done(((f32[1,1,16,64,128]{4,3,2,1,0:T(8,128)}), f32[2,1,16,64,128]{4,3,2,1,0:T(8,128)}) %all-gather.7.cloned.1.call-update) | async-done | bytes 1048592 | tf_op jit(solution)/shard_map/all_gather | solution.py:40
  276.1 2.1 fusion.42
  278.2 0.7 copy-done.4
  278.9 3.0 %add_multiply_fusion = f32[8,16,64,128]{3,2,1,0:T(8,128)} fusion(f32[8,16,64,128]{3,2,1,0:T(8,128)S(1)} %copy-done.4, f32[16,64,128]{2,1,0:T(8,128)S(1)} %fusion.42), kind=kLoop, calls=%fused_computation.106 | loop fusion | flops 2097152 | bytes 8912896 | tf_op jit(solution)/shard_map/div | solution.py:82
  (40 shorter events, 0.3 us)
Async XLA Ops:
  7.2 210.0 %all-gather.9.cloned.1.call-start = ((), (), s32[]{:S(2)}) async-start(), calls=%async_computation.2 | async-start | bytes 2621440 | tf_op jit(solution)/shard_map/all_gather | solution.py:40
  7.2 27.3 %copy-start.1 = (f32[8,16,64,128]{3,2,1,0:T(8,128)S(1)}, f32[8,16,64,128]{3,2,1,0:T(8,128)}, u32[]{:S(2)}) copy-start(f32[8,16,64,128]{3,2,1,0:T(8,128)} %param.3) | copy-start | bytes 12582916
  8.7 25.0 %collective-permute-start = (f32[1,16,64,128]{3,2,1,0:T(8,128)S(1)}, f32[1,16,64,128]{3,2,1,0:T(8,128)S(1)}, u32[]{:S(2)}, u32[]{:S(2)}) collective-permute-start(f32[1,16,64,128]{3,2,1,0:T(8,128)S(1)} %get-tuple-element.25), channel_id=1, source_target_pairs={{0,16},{16,32},{32,48},{48,64},{64,80},{80,96},{96,112},{112,128},... | collective-permute-start | bytes 1572872 | tf_op jit(solution)/shard_map/ppermute | solution.py:19
  11.3 14.8 %collective-permute-start.2 = (f32[8,1,64,128]{3,2,1,0:T(8,128)S(1)}, f32[8,1,64,128]{3,2,1,0:T(8,128)S(1)}, u32[]{:S(2)}, u32[]{:S(2)}) collective-permute-start(f32[8,1,64,128]{3,2,1,0:T(8,128)S(1)} %get-tuple-element.22), channel_id=1, source_target_pairs={{0,4},{4,8},{8,12},{12,0},{1,5},{5,9},{9,13},{13,1},{2,6},{6,10},{... | collective-permute-start | bytes 786440 | tf_op jit(solution)/shard_map/ppermute | solution.py:19
  14.7 15.8 %collective-permute-start.3 = (f32[8,1,64,128]{3,2,1,0:T(8,128)S(1)}, f32[8,1,64,128]{3,2,1,0:T(8,128)S(1)}, u32[]{:S(2)}, u32[]{:S(2)}) collective-permute-start(f32[8,1,64,128]{3,2,1,0:T(8,128)S(1)} %get-tuple-element.23), channel_id=1, source_target_pairs={{4,0},{8,4},{12,8},{0,12},{5,1},{9,5},{13,9},{1,13},{6,2},{10,6},{... | collective-permute-start | bytes 786440 | tf_op jit(solution)/shard_map/ppermute | solution.py:20
  17.8 19.4 %collective-permute-start.1 = (f32[1,16,64,128]{3,2,1,0:T(8,128)S(1)}, f32[1,16,64,128]{3,2,1,0:T(8,128)S(1)}, u32[]{:S(2)}, u32[]{:S(2)}) collective-permute-start(f32[1,16,64,128]{3,2,1,0:T(8,128)S(1)} %get-tuple-element.24), channel_id=1, source_target_pairs={{16,0},{32,16},{48,32},{64,48},{80,64},{96,80},{112,96},{128,112},... | collective-permute-start | bytes 1572872 | tf_op jit(solution)/shard_map/ppermute | solution.py:20
  24.1 14.0 %collective-permute-start.4 = (f32[8,16,1,128]{3,2,1,0:T(1,128)S(1)}, f32[8,16,1,128]{3,2,1,0:T(1,128)S(1)}, u32[]{:S(2)}, u32[]{:S(2)}) collective-permute-start(f32[8,16,1,128]{3,2,1,0:T(1,128)S(1)} %get-tuple-element.20), channel_id=1, source_target_pairs={{0,1},{1,2},{2,3},{3,0},{4,5},{5,6},{6,7},{7,4},{8,9},{9,10},{10,1... | collective-permute-start | bytes 196616 | tf_op jit(solution)/shard_map/ppermute | solution.py:19
  26.1 12.0 %collective-permute-start.5 = (f32[8,16,1,128]{3,2,1,0:T(1,128)S(1)}, f32[8,16,1,128]{3,2,1,0:T(1,128)S(1)}, u32[]{:S(2)}, u32[]{:S(2)}) collective-permute-start(f32[8,16,1,128]{3,2,1,0:T(1,128)S(1)} %get-tuple-element.21), channel_id=1, source_target_pairs={{1,0},{2,1},{3,2},{0,3},{5,4},{6,5},{7,6},{4,7},{9,8},{10,9},{11,1... | collective-permute-start | bytes 196616 | tf_op jit(solution)/shard_map/ppermute | solution.py:20
  34.5 3.8 %copy-start = (f32[8,16,64,128]{3,2,1,0:T(8,128)S(1)}, f32[8,16,64,128]{3,2,1,0:T(8,128)}, u32[]{:S(2)}) copy-start(f32[8,16,64,128]{3,2,1,0:T(8,128)} %param.5) | copy-start | bytes 12582916
  52.3 36.9 %copy-start.2 = (f32[8,16,64,128]{3,2,1,0:T(8,128)S(1)}, f32[8,16,64,128]{3,2,1,0:T(8,128)}, u32[]{:S(2)}) copy-start(f32[8,16,64,128]{3,2,1,0:T(8,128)} %fusion.34) | copy-start | bytes 12582916
  53.8 35.4 %collective-permute-start.6 = (f32[1,16,64,128]{3,2,1,0:T(8,128)S(1)}, f32[1,16,64,128]{3,2,1,0:T(8,128)S(1)}, u32[]{:S(2)}, u32[]{:S(2)}) collective-permute-start(f32[1,16,64,128]{3,2,1,0:T(8,128)S(1)} %get-tuple-element.16), channel_id=1, source_target_pairs={{0,16},{16,32},{32,48},{48,64},{64,80},{80,96},{96,112},{112,128},... | collective-permute-start | bytes 1572872 | tf_op jit(solution)/shard_map/ppermute | solution.py:19
  53.9 35.4 %collective-permute-start.7 = (f32[1,16,64,128]{3,2,1,0:T(8,128)S(1)}, f32[1,16,64,128]{3,2,1,0:T(8,128)S(1)}, u32[]{:S(2)}, u32[]{:S(2)}) collective-permute-start(f32[1,16,64,128]{3,2,1,0:T(8,128)S(1)} %get-tuple-element.17), channel_id=1, source_target_pairs={{16,0},{32,16},{48,32},{64,48},{80,64},{96,80},{112,96},{128,112},... | collective-permute-start | bytes 1572872 | tf_op jit(solution)/shard_map/ppermute | solution.py:20
  63.5 23.8 %collective-permute-start.8 = (f32[8,1,64,128]{3,2,1,0:T(8,128)S(1)}, f32[8,1,64,128]{3,2,1,0:T(8,128)S(1)}, u32[]{:S(2)}, u32[]{:S(2)}) collective-permute-start(f32[8,1,64,128]{3,2,1,0:T(8,128)S(1)} %get-tuple-element.18), channel_id=1, source_target_pairs={{0,4},{4,8},{8,12},{12,0},{1,5},{5,9},{9,13},{13,1},{2,6},{6,10},{... | collective-permute-start | bytes 786440 | tf_op jit(solution)/shard_map/ppermute | solution.py:19
  68.1 19.2 %collective-permute-start.9 = (f32[8,1,64,128]{3,2,1,0:T(8,128)S(1)}, f32[8,1,64,128]{3,2,1,0:T(8,128)S(1)}, u32[]{:S(2)}, u32[]{:S(2)}) collective-permute-start(f32[8,1,64,128]{3,2,1,0:T(8,128)S(1)} %get-tuple-element.19), channel_id=1, source_target_pairs={{4,0},{8,4},{12,8},{0,12},{5,1},{9,5},{13,9},{1,13},{6,2},{10,6},{... | collective-permute-start | bytes 786440 | tf_op jit(solution)/shard_map/ppermute | solution.py:20
  69.4 18.0 %collective-permute-start.10 = (f32[8,16,1,128]{3,2,1,0:T(1,128)S(1)}, f32[8,16,1,128]{3,2,1,0:T(1,128)S(1)}, u32[]{:S(2)}, u32[]{:S(2)}) collective-permute-start(f32[8,16,1,128]{3,2,1,0:T(1,128)S(1)} %get-tuple-element.14), channel_id=1, source_target_pairs={{0,1},{1,2},{2,3},{3,0},{4,5},{5,6},{6,7},{7,4},{8,9},{9,10},{10,1... | collective-permute-start | bytes 196616 | tf_op jit(solution)/shard_map/ppermute | solution.py:19
  87.3 1.9 collective-permute-start.11
  97.3 35.5 %collective-permute-start.12 = (f32[1,16,64,128]{3,2,1,0:T(8,128)S(1)}, f32[1,16,64,128]{3,2,1,0:T(8,128)S(1)}, u32[]{:S(2)}, u32[]{:S(2)}) collective-permute-start(f32[1,16,64,128]{3,2,1,0:T(8,128)S(1)} %get-tuple-element.10), channel_id=1, source_target_pairs={{0,16},{16,32},{32,48},{48,64},{64,80},{80,96},{96,112},{112,128},... | collective-permute-start | bytes 1572872 | tf_op jit(solution)/shard_map/ppermute | solution.py:19
  97.4 35.4 %collective-permute-start.13 = (f32[1,16,64,128]{3,2,1,0:T(8,128)S(1)}, f32[1,16,64,128]{3,2,1,0:T(8,128)S(1)}, u32[]{:S(2)}, u32[]{:S(2)}) collective-permute-start(f32[1,16,64,128]{3,2,1,0:T(8,128)S(1)} %get-tuple-element.11), channel_id=1, source_target_pairs={{16,0},{32,16},{48,32},{64,48},{80,64},{96,80},{112,96},{128,112},... | collective-permute-start | bytes 1572872 | tf_op jit(solution)/shard_map/ppermute | solution.py:20
  104.0 26.4 %collective-permute-start.14 = (f32[8,1,64,128]{3,2,1,0:T(8,128)S(1)}, f32[8,1,64,128]{3,2,1,0:T(8,128)S(1)}, u32[]{:S(2)}, u32[]{:S(2)}) collective-permute-start(f32[8,1,64,128]{3,2,1,0:T(8,128)S(1)} %get-tuple-element.12), channel_id=1, source_target_pairs={{0,4},{4,8},{8,12},{12,0},{1,5},{5,9},{9,13},{13,1},{2,6},{6,10},{... | collective-permute-start | bytes 786440 | tf_op jit(solution)/shard_map/ppermute | solution.py:19
  105.3 25.7 %collective-permute-start.15 = (f32[8,1,64,128]{3,2,1,0:T(8,128)S(1)}, f32[8,1,64,128]{3,2,1,0:T(8,128)S(1)}, u32[]{:S(2)}, u32[]{:S(2)}) collective-permute-start(f32[8,1,64,128]{3,2,1,0:T(8,128)S(1)} %get-tuple-element.13), channel_id=1, source_target_pairs={{4,0},{8,4},{12,8},{0,12},{5,1},{9,5},{13,9},{1,13},{6,2},{10,6},{... | collective-permute-start | bytes 786440 | tf_op jit(solution)/shard_map/ppermute | solution.py:20
  108.3 22.7 %collective-permute-start.16 = (f32[8,16,1,128]{3,2,1,0:T(1,128)S(1)}, f32[8,16,1,128]{3,2,1,0:T(1,128)S(1)}, u32[]{:S(2)}, u32[]{:S(2)}) collective-permute-start(f32[8,16,1,128]{3,2,1,0:T(1,128)S(1)} %get-tuple-element.8), channel_id=1, source_target_pairs={{0,1},{1,2},{2,3},{3,0},{4,5},{5,6},{6,7},{7,4},{8,9},{9,10},{10,1... | collective-permute-start | bytes 196616 | tf_op jit(solution)/shard_map/ppermute | solution.py:19
  130.4 2.4 collective-permute-start.17
  141.0 29.9 %collective-permute-start.18 = (f32[1,16,64,128]{3,2,1,0:T(8,128)S(1)}, f32[1,16,64,128]{3,2,1,0:T(8,128)S(1)}, u32[]{:S(2)}, u32[]{:S(2)}) collective-permute-start(f32[1,16,64,128]{3,2,1,0:T(8,128)S(1)} %get-tuple-element.4), channel_id=1, source_target_pairs={{0,16},{16,32},{32,48},{48,64},{64,80},{80,96},{96,112},{112,128},... | collective-permute-start | bytes 1572872 | tf_op jit(solution)/shard_map/ppermute | solution.py:19
  141.1 29.8 %collective-permute-start.19 = (f32[1,16,64,128]{3,2,1,0:T(8,128)S(1)}, f32[1,16,64,128]{3,2,1,0:T(8,128)S(1)}, u32[]{:S(2)}, u32[]{:S(2)}) collective-permute-start(f32[1,16,64,128]{3,2,1,0:T(8,128)S(1)} %get-tuple-element.5), channel_id=1, source_target_pairs={{16,0},{32,16},{48,32},{64,48},{80,64},{96,80},{112,96},{128,112},... | collective-permute-start | bytes 1572872 | tf_op jit(solution)/shard_map/ppermute | solution.py:20
  147.7 19.4 %collective-permute-start.20 = (f32[8,1,64,128]{3,2,1,0:T(8,128)S(1)}, f32[8,1,64,128]{3,2,1,0:T(8,128)S(1)}, u32[]{:S(2)}, u32[]{:S(2)}) collective-permute-start(f32[8,1,64,128]{3,2,1,0:T(8,128)S(1)} %get-tuple-element.6), channel_id=1, source_target_pairs={{0,4},{4,8},{8,12},{12,0},{1,5},{5,9},{9,13},{13,1},{2,6},{6,10},{... | collective-permute-start | bytes 786440 | tf_op jit(solution)/shard_map/ppermute | solution.py:19
  148.1 21.0 %collective-permute-start.21 = (f32[8,1,64,128]{3,2,1,0:T(8,128)S(1)}, f32[8,1,64,128]{3,2,1,0:T(8,128)S(1)}, u32[]{:S(2)}, u32[]{:S(2)}) collective-permute-start(f32[8,1,64,128]{3,2,1,0:T(8,128)S(1)} %get-tuple-element.7), channel_id=1, source_target_pairs={{4,0},{8,4},{12,8},{0,12},{5,1},{9,5},{13,9},{1,13},{6,2},{10,6},{... | collective-permute-start | bytes 786440 | tf_op jit(solution)/shard_map/ppermute | solution.py:20
  152.0 17.1 %collective-permute-start.22 = (f32[8,16,1,128]{3,2,1,0:T(1,128)S(1)}, f32[8,16,1,128]{3,2,1,0:T(1,128)S(1)}, u32[]{:S(2)}, u32[]{:S(2)}) collective-permute-start(f32[8,16,1,128]{3,2,1,0:T(1,128)S(1)} %get-tuple-element.2), channel_id=1, source_target_pairs={{0,1},{1,2},{2,3},{3,0},{4,5},{5,6},{6,7},{7,4},{8,9},{9,10},{10,1... | collective-permute-start | bytes 196616 | tf_op jit(solution)/shard_map/ppermute | solution.py:19
  167.1 3.8 %collective-permute-start.23 = (f32[8,16,1,128]{3,2,1,0:T(1,128)S(1)}, f32[8,16,1,128]{3,2,1,0:T(1,128)S(1)}, u32[]{:S(2)}, u32[]{:S(2)}) collective-permute-start(f32[8,16,1,128]{3,2,1,0:T(1,128)S(1)} %get-tuple-element.3), channel_id=1, source_target_pairs={{1,0},{2,1},{3,2},{0,3},{5,4},{6,5},{7,6},{4,7},{9,8},{10,9},{11,1... | collective-permute-start | bytes 196616 | tf_op jit(solution)/shard_map/ppermute | solution.py:20
  179.0 5.4 %copy-start.5 = (f32[8,16,64,128]{3,2,1,0:T(8,128)}, f32[8,16,64,128]{3,2,1,0:T(8,128)S(1)}, u32[]{:S(2)}) copy-start(f32[8,16,64,128]{3,2,1,0:T(8,128)S(1)} %fusion.4) | copy-start | bytes 12582916
  184.4 2.0 copy-start.3
  187.3 59.8 %all-gather.5.cloned.1.call-start = ((), (), s32[]{:S(2)}) async-start(), calls=%async_computation | async-start | bytes 1572864 | tf_op jit(solution)/shard_map/all_gather | solution.py:40
  217.2 58.9 %copy-start.6 = (f32[4,16,64,128]{3,2,1,0:T(8,128)S(1)}, f32[4,16,64,128]{3,2,1,0:T(8,128)}, u32[]{:S(2)}) copy-start(f32[4,16,64,128]{3,2,1,0:T(8,128)} %all-gather.9.cloned.1.call-done) | copy-start | bytes 6291460
  219.9 56.2 %all-gather.7.cloned.1.call-start = ((), (), s32[]{:S(2)}) async-start(), calls=%async_computation.1 | async-start | bytes 1572864 | tf_op jit(solution)/shard_map/all_gather | solution.py:40
  276.1 2.8 copy-start.4
Sparse Core Ops, SparseCore 0:
  187.4 29.7 all-gather.8
  220.0 27.0 all-gather.4
  249.3 26.7 all-gather.6
where the time goes:
time: 289 us; the launch traced here: 288 us
  waiting for transfers between devices  149 us (52%)
  starting transfers between devices  54.9 us (19%)
  other arithmetic  53.3 us (18%)
  local copies, waits for them, and re-layouts  17.2 us (6%)
  between operations  14.1 us (5%)
    all_gather x3, waiting for transfers between devices, prefix_by_axis(): pieces = lax.all_gather(so_far, axis)  83.9 us
    ppermute x12, waiting for transfers between devices, padded_2(): lax.ppermute(last, axis, up)  55.1 us
    ppermute x12, starting transfers between devices, padded_2(): lax.ppermute(initial, axis, [(b, a) for a, b in up])  39 us
    add x4, other arithmetic, march_step(): return 2.0 * middle - before + speed_square * spread  38 us
    ppermute x12, starting transfers between devices, padded_2(): lax.ppermute(last, axis, up)  15.7 us
    ppermute x12, waiting for transfers between devices, padded_2(): lax.ppermute(initial, axis, [(b, a) for a, b in up])  9.91 us
    add x3, other arithmetic, add_pair(): return earlier_total + later_total  6.85 us
    slice x11, local copies, waits for them, and re-layouts, padded_2(): last = lax.slice_in_dim(value, length - width, length, axis=dim)  6.65 us
  transfers between devices with their start and end apart: 27, of which 12 were waited for; matrix products, arithmetic and copies ran while one was open for 4% of the time, Pallas kernels for 0%

commit v1 on v0

v1 whole, which is shorter than its diff:
```python
import functools

import jax
import jax.numpy as jnp
from jax import lax
from jax.experimental import pallas as pl
from jax.experimental.pallas import tpu as pltpu
from jax.sharding import PartitionSpec as P

STEPS = 4
MESH = pl.DeviceIdType.MESH
PAD = 8
CHUNKS = 4
ORDER = (0, 3, 1, 2)
JUP, JDOWN, IUP, IDOWN = range(4)


def march_kernel(
    sizes, u_hbm, e_hbm, c_hbm, end_hbm, below_hbm,
    field, speed, k_out, k_in, total, gathered, prefix,
    load_sem, send_sem, recv_sem, k_send_sem, k_recv_sem,
    out_sem, own_sem, t_send_sem, t_recv_sem, p_send_sem, p_recv_sem,
):
    ny, nx, nz = sizes
    nj, ni, nk, _ = u_hbm.shape
    kc = nk // CHUNKS
    y, x, z = lax.axis_index("py"), lax.axis_index("px"), lax.axis_index("pz")
    up = {"py": lax.rem(y + 1, ny), "px": lax.rem(x + 1, nx), "pz": lax.rem(z + 1, nz)}
    down = {"py": lax.rem(y + ny - 1, ny), "px": lax.rem(x + nx - 1, nx), "pz": lax.rem(z + nz - 1, nz)}

    def inner(piece):
        return pl.ds(piece * kc, kc)

    def padded(piece, shift=0):
        return pl.ds(PAD + piece * kc + shift, kc)

    def load(which, piece):
        block = (pl.ds(1, nj), pl.ds(1, ni), padded(piece))
        cells = (slice(None), slice(None), inner(piece))
        source = (u_hbm, e_hbm, c_hbm)[which].at[cells]
        target = speed.at[cells] if which == 2 else field.at[(which, *block)]
        return pltpu.make_async_copy(source, target, load_sem.at[which, piece])

    def face(step, piece, side):
        slot = step % 2
        rows = padded(piece)
        i_all, j_all = pl.ds(1, ni), pl.ds(1, nj)
        here = {
            JUP: (slot, nj, i_all, rows),
            JDOWN: (slot, 1, i_all, rows),
            IUP: (slot, j_all, ni, rows),
            IDOWN: (slot, j_all, 1, rows),
        }[side]
        there = {
            JUP: (slot, 0, i_all, rows),
            JDOWN: (slot, nj + 1, i_all, rows),
            IUP: (slot, j_all, 0, rows),
            IDOWN: (slot, j_all, ni + 1, rows),
        }[side]
        axis = "py" if side in (JUP, JDOWN) else "px"
        to = (up if side in (JUP, IUP) else down)[axis]
        if step == 0:
            rows = inner(piece)
            source = u_hbm.at[
                {
                    JUP: (nj - 1, slice(None), rows),
                    JDOWN: (0, slice(None), rows),
                    IUP: (slice(None), ni - 1, rows),
                    IDOWN: (slice(None), 0, rows),
                }[side]
            ]
        else:
            source = field.at[here]
        return pltpu.make_async_remote_copy(
            src_ref=source, dst_ref=field.at[there],
            send_sem=send_sem.at[step, piece, side], recv_sem=recv_sem.at[step, piece, side],
            device_id={axis: to}, device_id_type=MESH,
        )

    def k_face(step, high):
        return pltpu.make_async_remote_copy(
            src_ref=k_out.at[step % 2, high], dst_ref=k_in.at[step % 2, high],
            send_sem=k_send_sem.at[step, high], recv_sem=k_recv_sem.at[step, high],
            device_id={"pz": (up if high else down)["pz"]}, device_id_type=MESH,
        )

    def send_k_face(step, high):
        slot = step % 2
        row = PAD + (nk - 1 if high else 0)

        def gather(j, _):
            for i in range(ni):
                k_out[slot, high, j, pl.ds(i, 1)] = field[slot, j + 1, i + 1, pl.ds(row, 1)]
            return 0

        lax.fori_loop(0, nj, gather, 0)
        k_face(step, high).start()

    def take_k_face(step, high):
        slot = step % 2
        row = PAD - 1 if high else PAD + nk
        k_face(step, high).wait_recv()

        def scatter(j, _):
            for i in range(ni):
                field[slot, j + 1, i + 1, pl.ds(row, 1)] = k_in[slot, high, j, pl.ds(i, 1)]
            return 0

        lax.fori_loop(0, nj, scatter, 0)

    def advance(step, piece):
        now, later = step % 2, (step + 1) % 2
        rows = padded(piece)
        lower, upper = padded(piece, -1), padded(piece, 1)

        def column(i, _):
            cells = [field[now, j, i + 1, rows] for j in range(nj + 2)]
            amount = None
            for j in range(1, nj + 1):
                middle = cells[j]
                spread = cells[j - 1] + cells[j + 1]
                spread = spread + (field[now, j, i, rows] + field[now, j, i + 2, rows])
                spread = spread + (field[now, j, i + 1, lower] + field[now, j, i + 1, upper])
                spread = spread - 6.0 * middle
                value = 2.0 * middle - field[later, j, i + 1, rows] + speed[j - 1, i, inner(piece)] * spread
                field[later, j, i + 1, rows] = value
                amount = value if amount is None else amount + value
            if step == STEPS - 1:
                total[i, inner(piece)] = amount
            return 0

        lax.fori_loop(0, ni, column, 0)

    def end_copy(piece):
        return pltpu.make_async_copy(
            field.at[STEPS % 2, pl.ds(1, nj), pl.ds(1, ni), padded(piece)], end_hbm.at[:, :, inner(piece)], out_sem.at[piece]
        )

    def total_copy(piece, away):
        to = lax.rem(y + away, ny)
        return pltpu.make_async_remote_copy(
            src_ref=total.at[to, inner(piece)], dst_ref=gathered.at[piece, y],
            send_sem=t_send_sem.at[piece], recv_sem=t_recv_sem.at[piece],
            device_id={"py": to}, device_id_type=MESH,
        )

    def prefix_copy(piece, away):
        to = lax.rem(y + away, ny)
        return pltpu.make_async_remote_copy(
            src_ref=prefix.at[piece, to], dst_ref=below_hbm.at[y, inner(piece)],
            send_sem=p_send_sem.at[piece], recv_sem=p_recv_sem.at[piece],
            device_id={"py": to}, device_id_type=MESH,
        )

    def own_prefix(piece):
        return pltpu.make_async_copy(prefix.at[piece, y], below_hbm.at[y, inner(piece)], own_sem.at[piece])

    def others(sem):
        return pltpu.make_async_copy(gathered.at[0, pl.ds(0, ny - 1)], gathered.at[0, pl.ds(0, ny - 1)], sem)

    def to_all(copy, piece):
        def one(away, _):
            copy(piece, away).start()
            return 0

        lax.fori_loop(1, ny, one, 0)

    def send_totals(piece):
        to_all(total_copy, piece)

    def send_prefixes(piece):
        others(t_recv_sem.at[piece]).wait()
        gathered[piece, y] = total[y, inner(piece)]

        def add(n, so_far):
            prefix[piece, n] = so_far
            return so_far + gathered[piece, n]

        lax.fori_loop(0, ny, add, jnp.zeros(gathered.shape[2:], jnp.float32))
        to_all(prefix_copy, piece)
        own_prefix(piece).start()

    for piece in ORDER:
        load(0, piece).start()
    barrier = pltpu.get_barrier_semaphore()

    def greet(away, _):
        pl.semaphore_signal(barrier, inc=1, device_id={"py": lax.rem(y + away, ny)}, device_id_type=MESH)
        return 0

    for axis in ("px", "pz"):
        for near in (up, down):
            pl.semaphore_signal(barrier, inc=1, device_id={axis: near[axis]}, device_id_type=MESH)
    lax.fori_loop(1, ny, greet, 0)
    pl.semaphore_wait(barrier, ny - 1 + 4)

    for piece in ORDER:
        for side in range(4):
            face(0, piece, side).start()
    for piece in ORDER:
        for which in (1, 2):
            load(which, piece).start()
    for piece in ORDER:
        load(0, piece).wait()
        if piece == 0:
            send_k_face(0, 0)
        if piece == CHUNKS - 1:
            send_k_face(0, 1)

    for step in range(STEPS):
        for at, piece in enumerate(ORDER):
            if step == 0:
                for which in (1, 2):
                    load(which, piece).wait()
            if piece == 0:
                take_k_face(step, 1)
            if piece == CHUNKS - 1:
                take_k_face(step, 0)
            for side in range(4):
                if step >= 1:
                    face(step - 1, piece, side).wait_send()
                face(step, piece, side).wait_recv()
            advance(step, piece)
            if step < STEPS - 1:
                for side in range(4):
                    face(step + 1, piece, side).start()
                for high, owner in ((0, 0), (1, CHUNKS - 1)):
                    if piece == owner:
                        if step >= 1:
                            k_face(step - 1, high).wait_send()
                        send_k_face(step + 1, high)
            else:
                end_copy(piece).start()
                send_totals(piece)
                if at >= 2:
                    send_prefixes(ORDER[at - 2])
    for piece in ORDER[2:]:
        send_prefixes(piece)
    for piece in ORDER:
        for side in range(4):
            face(STEPS - 1, piece, side).wait_send()
        end_copy(piece).wait()
        own_prefix(piece).wait()
        others(t_send_sem.at[piece]).wait()
        others(p_send_sem.at[piece]).wait()
        others(p_recv_sem.at[piece]).wait()
    for step in (STEPS - 2, STEPS - 1):
        for high in (0, 1):
            k_face(step, high).wait_send()


def sums_kernel(scale, field_ref, below_ref, sums_ref, end_ref):
    so_far = below_ref[...]
    for j in range(field_ref.shape[0]):
        value = field_ref[j]
        end_ref[j] = value
        so_far = so_far + value
        sums_ref[j] = so_far * scale


def local(sizes, field_now, earlier, speed_square):
    nj, ni, nk, lanes = field_now.shape
    kc = nk // CHUNKS
    f32 = jnp.float32
    dma = pltpu.SemaphoreType.DMA
    end, below = pl.pallas_call(
        functools.partial(march_kernel, sizes),
        out_shape=(jax.ShapeDtypeStruct(field_now.shape, f32), jax.ShapeDtypeStruct((ni, nk, lanes), f32)),
        in_specs=[pl.BlockSpec(memory_space=pl.ANY)] * 3,
        out_specs=[pl.BlockSpec(memory_space=pl.ANY)] * 2,
        scratch_shapes=[
            pltpu.VMEM((2, nj + 2, ni + 2, nk + 2 * PAD, lanes), f32),
            pltpu.VMEM((nj, ni, nk, lanes), f32),
            pltpu.VMEM((2, 2, nj, ni, lanes), f32),
            pltpu.VMEM((2, 2, nj, ni, lanes), f32),
            pltpu.VMEM((ni, nk, lanes), f32),
            pltpu.VMEM((CHUNKS, ni, kc, lanes), f32),
            pltpu.VMEM((CHUNKS, ni, kc, lanes), f32),
            dma((3, CHUNKS)),
            dma((STEPS, CHUNKS, 4)),
            dma((STEPS, CHUNKS, 4)),
            dma((STEPS, 2)),
            dma((STEPS, 2)),
            dma((CHUNKS,)),
            dma((CHUNKS,)),
            dma((CHUNKS,)),
            dma((CHUNKS,)),
            dma((CHUNKS,)),
            dma((CHUNKS,)),
        ],
        compiler_params=pltpu.CompilerParams(
            collective_id=0, has_side_effects=True, vmem_limit_bytes=48 * 1024 * 1024
        ),
        name="march",
    )(field_now, earlier, speed_square)
    rows = 2
    block = pl.BlockSpec((nj, rows, nk, lanes), lambda n: (0, n, 0, 0))
    sums, end = pl.pallas_call(
        functools.partial(sums_kernel, 1.0 / (nj * sizes[0])),
        grid=(ni // rows,),
        out_shape=(jax.ShapeDtypeStruct(field_now.shape, f32),) * 2,
        in_specs=[block, pl.BlockSpec((rows, nk, lanes), lambda n: (n, 0, 0))],
        out_specs=[block, block],
        name="sums",
    )(end, below)
    return sums, end


def solution(mesh):
    spec = P("py", "px", "pz", None)
    sizes = tuple(mesh.shape[axis] for axis in ("py", "px", "pz"))
    return jax.shard_map(
        functools.partial(local, sizes),
        mesh=mesh,
        in_specs=(spec, spec, spec),
        out_specs=(spec, spec),
        check_vma=False,
    )
```

time: 289 us -> 153 us (0.53)
  Pallas kernels: 0 us -> 149 us
  waiting for transfers between devices: 149 us -> 0 us
  starting transfers between devices: 54.9 us -> 0 us
  other arithmetic: 53.3 us -> 0 us
  local copies, waits for them, and re-layouts: 17.2 us -> 2.72 us
  between operations: 14.1 us -> 0.65 us
    pallas_call x0 -> x2, Pallas kernels: none -> 149 us  [the longest x1 142 us: local(): pl.pallas_call(functools.partial(march_kernel, sizes), out_shape=(jax.Sha...]
    all_gather x3 -> x0, waiting for transfers between devices: 83.9 us -> none  [prefix_by_axis(): pieces = lax.all_gather(so_far, axis)]
    ppermute x24 -> x0, waiting for transfers between devices: 65 us -> none  [the longest x12 55.1 us: padded_2(): lax.ppermute(last, axis, up)]
    ppermute x24 -> x0, starting transfers between devices: 54.8 us -> none  [the longest x12 39 us: padded_2(): lax.ppermute(initial, axis, [(b, a) for a, b in up])]
    add x7 -> x0, other arithmetic: 44.9 us -> none  [the longest x4 38 us: march_step(): return 2.0 * middle - before + speed_square * spread]
    slice x13 -> x0, local copies, waits for them, and re-layouts: 8.93 us -> none  [the longest x11 6.65 us: padded_2(): last = lax.slice_in_dim(value, length - width, length, axis=dim)]
    another operation x1 -> x0, other arithmetic: 5.41 us -> none  [local(): here = jnp.cumsum(field_now, axis=0)]
    unnamed x16 -> x4, local copies, waits for them, and re-layouts: 6.47 us -> 2.72 us
  transfers between devices with their start and end apart: 27 -> 0, of which waited for: 12 -> 0; matrix products, arithmetic and copies ran while one was open for 4% -> 0% of each run, Pallas kernels for 0% -> 0%
where the time goes in v1:
time: 153 us
  Pallas kernels  149 us (97%)
  local copies, waits for them, and re-layouts  2.72 us (2%)
    pallas_call x1, Pallas kernels, local(): pl.pallas_call(functools.partial(march_kernel, sizes), out_shape=(jax.Sha...  142 us
    pallas_call x1, Pallas kernels, local(): pl.pallas_call(functools.partial(sums_kernel, 1.0 / (nj * sizes[0])), gri...  7.32 us

profile of v1, /device:TPU:8, one launch (start us, length us, event | category | flops | bytes accessed | tf_op | source)
XLA Modules:
  0.0 152.5 jit_solution(11869941261314843483)
XLA Ops:
  0.6 141.8 %march.1 = (f32[8,16,64,128]{3,2,1,0:T(8,128)S(1)}, f32[16,64,128]{2,1,0:T(8,128)S(1)}) custom-call(f32[8,16,64,128]{3,2,1,0:T(8,128)} %u_hbm.1, f32[8,16,64,128]{3,2,1,0:T(8,128)} %e_hbm.1, f32[8,16,64,128]{3,2,1,0:T(8,128)} %c_hbm.1), custom_call_target="tpu_custom_call" | custom-call | tf_op jit(solution)/shard_map/march/pallas_call | solution.py:266
  142.5 0.0 copy-start
  142.5 1.9 %copy-done = f32[8,16,64,128]{3,2,1,0:T(8,128)} copy-done((f32[8,16,64,128]{3,2,1,0:T(8,128)}, f32[8,16,64,128]{3,2,1,0:T(8,128)S(1)}, u32[]{:S(2)}) %copy-start) | copy-done | bytes 4194328
  144.4 0.0 copy-start.1
  144.4 0.8 copy-done.1
  145.2 7.3 %sums.1 = (f32[8,16,64,128]{3,2,1,0:T(8,128)}, f32[8,16,64,128]{3,2,1,0:T(8,128)}) custom-call(f32[8,16,64,128]{3,2,1,0:T(8,128)} %copy-done, f32[16,64,128]{2,1,0:T(8,128)} %copy-done.1), custom_call_target="tpu_custom_call" | custom-call | tf_op jit(solution)/shard_map/sums/pallas_call | solution.py:298
Async XLA Ops:
  142.5 1.9 %copy-start = (f32[8,16,64,128]{3,2,1,0:T(8,128)}, f32[8,16,64,128]{3,2,1,0:T(8,128)S(1)}, u32[]{:S(2)}) copy-start(f32[8,16,64,128]{3,2,1,0:T(8,128)S(1)} %get-tuple-element.4.field_ref) | copy-start | bytes 12582916
  144.4 0.8 copy-start.1

commit v2 on v1

--- a/solution.py
+++ b/solution.py
@@ -12,13 +12,14 @@
 PAD = 8
 CHUNKS = 4
 ORDER = (0, 3, 1, 2)
-JUP, JDOWN, IUP, IDOWN = range(4)
+JUP, JDOWN, IUP, IDOWN = SIDES = range(4)
+STRAIGHT, ROUND, BESIDE = PARTS = ((0, 5), (5, 6), (11, 5))
 
 
 def march_kernel(
     sizes, u_hbm, e_hbm, c_hbm, end_hbm, below_hbm,
-    field, speed, k_out, k_in, total, gathered, prefix,
-    load_sem, send_sem, recv_sem, k_send_sem, k_recv_sem,
+    field, speed, k_out, k_in, total, gathered, prefix, passing,
+    load_sem, send_sem, recv_sem, k_send_sem, k_recv_sem, pass_send_sem, pass_recv_sem,
     out_sem, own_sem, t_send_sem, t_recv_sem, p_send_sem, p_recv_sem,
 ):
     ny, nx, nz = sizes
@@ -41,41 +42,79 @@
         target = speed.at[cells] if which == 2 else field.at[(which, *block)]
         return pltpu.make_async_copy(source, target, load_sem.at[which, piece])
 
-    def face(step, piece, side):
+    run, half = ny // 2, ny // 4
+    place = lax.rem(y, run)
+    ends = {JUP: place == run - 1, JDOWN: place == 0}
+    away = {(JUP, ROUND): 1 - half, (JUP, BESIDE): -1, (JDOWN, ROUND): half - 1, (JDOWN, BESIDE): 1}
+
+    def face(step, piece, side, part=None, passed=False):
         slot = step % 2
         rows = padded(piece)
-        i_all, j_all = pl.ds(1, ni), pl.ds(1, nj)
-        here = {
-            JUP: (slot, nj, i_all, rows),
-            JDOWN: (slot, 1, i_all, rows),
-            IUP: (slot, j_all, ni, rows),
-            IDOWN: (slot, j_all, 1, rows),
-        }[side]
-        there = {
-            JUP: (slot, 0, i_all, rows),
-            JDOWN: (slot, nj + 1, i_all, rows),
-            IUP: (slot, j_all, 0, rows),
-            IDOWN: (slot, j_all, ni + 1, rows),
-        }[side]
-        axis = "py" if side in (JUP, JDOWN) else "px"
-        to = (up if side in (JUP, IUP) else down)[axis]
+        first, count = part or (0, ni)
+        i_all, j_all = pl.ds(1 + first, count), pl.ds(1, nj)
+        along_j, high = side in (JUP, JDOWN), side in (JUP, IUP)
+        if along_j:
+            here = (slot, nj if high else 1, i_all, rows)
+            there = (slot, 0 if high else nj + 1, i_all, rows)
+        else:
+            here = (slot, j_all, ni if high else 1, rows)
+            there = (slot, j_all, 0 if high else ni + 1, rows)
+        axis = "py" if along_j else "px"
+        to = (up if high else down)[axis]
+        source, target = field.at[here], field.at[there]
+        arrived = recv_sem.at[step, piece, side]
         if step == 0:
             rows = inner(piece)
-            source = u_hbm.at[
-                {
-                    JUP: (nj - 1, slice(None), rows),
-                    JDOWN: (0, slice(None), rows),
-                    IUP: (slice(None), ni - 1, rows),
-                    IDOWN: (slice(None), 0, rows),
-                }[side]
-            ]
-        else:
-            source = field.at[here]
-        return pltpu.make_async_remote_copy(
-            src_ref=source, dst_ref=field.at[there],
-            send_sem=send_sem.at[step, piece, side], recv_sem=recv_sem.at[step, piece, side],
+            if along_j:
+                source = u_hbm.at[nj - 1 if high else 0, pl.ds(first, count), rows]
+            else:
+                source = u_hbm.at[:, ni - 1 if high else 0, rows]
+        if passed:
+            to = y + away[side, part]
+            target, arrived = passing.at[step, piece, pl.ds(0, count)], pass_recv_sem.at[step, piece]
+        return pltpu.make_async_remote_copy(
+            src_ref=source, dst_ref=target, send_sem=send_sem.at[step, piece, side], recv_sem=arrived,
             device_id={axis: to}, device_id_type=MESH,
         )
+
+    def pass_on(step, piece, side, part):
+        first, count = part
+        high = side == JUP
+        to = lax.rem(y - away[side, part] + (1 if high else ny - 1), ny)
+        there = (step % 2, 0 if high else nj + 1, pl.ds(1 + first, count), padded(piece))
+        return pltpu.make_async_remote_copy(
+            src_ref=passing.at[step, piece, pl.ds(0, count)], dst_ref=field.at[there],
+            send_sem=pass_send_sem.at[step, piece], recv_sem=recv_sem.at[step, piece, side],
+            device_id={"py": to}, device_id_type=MESH,
+        )
+
+    def send_faces(step, piece):
+        for side in SIDES:
+            if side not in ends:
+                face(step, piece, side).start()
+                continue
+
+            @pl.when(ends[side])
+            def _():
+                for part in (ROUND, BESIDE):
+                    face(step, piece, side, part, passed=True).start()
+                face(step, piece, side, STRAIGHT).start()
+
+            @pl.when(jnp.logical_not(ends[side]))
+            def _():
+                face(step, piece, side).start()
+
+    def as_relay(act):
+        for (side, part), steps in away.items():
+            at = (run - 1 if side == JUP else 0) + steps
+            pl.when(place == at)(functools.partial(act, side, part))
+
+    def relay(step, piece):
+        def act(side, part):
+            face(step, piece, side, part, passed=True).wait_recv()
+            pass_on(step, piece, side, part).start()
+
+        as_relay(act)
 
     def k_face(step, high):
         return pltpu.make_async_remote_copy(
@@ -195,8 +234,7 @@
     pl.semaphore_wait(barrier, ny - 1 + 4)
 
     for piece in ORDER:
-        for side in range(4):
-            face(0, piece, side).start()
+        send_faces(0, piece)
     for piece in ORDER:
         for which in (1, 2):
             load(which, piece).start()
@@ -216,14 +254,14 @@
                 take_k_face(step, 1)
             if piece == CHUNKS - 1:
                 take_k_face(step, 0)
-            for side in range(4):
+            relay(step, piece)
+            for side in SIDES:
                 if step >= 1:
                     face(step - 1, piece, side).wait_send()
                 face(step, piece, side).wait_recv()
             advance(step, piece)
             if step < STEPS - 1:
-                for side in range(4):
-                    face(step + 1, piece, side).start()
+                send_faces(step + 1, piece)
                 for high, owner in ((0, 0), (1, CHUNKS - 1)):
                     if piece == owner:
                         if step >= 1:
@@ -237,7 +275,7 @@
     for piece in ORDER[2:]:
         send_prefixes(piece)
     for piece in ORDER:
-        for side in range(4):
+        for side in SIDES:
             face(STEPS - 1, piece, side).wait_send()
         end_copy(piece).wait()
         own_prefix(piece).wait()
@@ -248,14 +286,38 @@
         for high in (0, 1):
             k_face(step, high).wait_send()
 
-
-def sums_kernel(scale, field_ref, below_ref, sums_ref, end_ref):
-    so_far = below_ref[...]
-    for j in range(field_ref.shape[0]):
-        value = field_ref[j]
-        end_ref[j] = value
-        so_far = so_far + value
-        sums_ref[j] = so_far * scale
+    def passed_on(side, part):
+        for step in range(STEPS):
+            for piece in ORDER:
+                pass_on(step, piece, side, part).wait_send()
+
+    as_relay(passed_on)
+
+
+def sums_kernel(scale, field_ref, below_ref, sums_hbm, end_hbm, sums, sem):
+    nj, ni = field_ref.shape[:2]
+    ends = pltpu.make_async_copy(field_ref, end_hbm, sem.at[ni])
+    ends.start()
+
+    def put(i):
+        return pltpu.make_async_copy(sums.at[:, i], sums_hbm.at[:, i], sem.at[i])
+
+    def row(i, _):
+        so_far = below_ref[i]
+        for j in range(nj):
+            so_far = so_far + field_ref[j, i]
+            sums[j, i] = so_far * scale
+        put(i).start()
+        return 0
+
+    lax.fori_loop(0, ni, row, 0)
+
+    def written(i, _):
+        put(i).wait()
+        return 0
+
+    lax.fori_loop(0, ni, written, 0)
+    ends.wait()
 
 
 def local(sizes, field_now, earlier, speed_square):
@@ -276,11 +338,14 @@
             pltpu.VMEM((ni, nk, lanes), f32),
             pltpu.VMEM((CHUNKS, ni, kc, lanes), f32),
             pltpu.VMEM((CHUNKS, ni, kc, lanes), f32),
+            pltpu.VMEM((STEPS, CHUNKS, max(ROUND[1], BESIDE[1]), kc, lanes), f32),
             dma((3, CHUNKS)),
-            dma((STEPS, CHUNKS, 4)),
-            dma((STEPS, CHUNKS, 4)),
+            dma((STEPS, CHUNKS, len(SIDES))),
+            dma((STEPS, CHUNKS, len(SIDES))),
             dma((STEPS, 2)),
             dma((STEPS, 2)),
+            dma((STEPS, CHUNKS)),
+            dma((STEPS, CHUNKS)),
             dma((CHUNKS,)),
             dma((CHUNKS,)),
             dma((CHUNKS,)),
@@ -293,14 +358,13 @@
         ),
         name="march",
     )(field_now, earlier, speed_square)
-    rows = 2
-    block = pl.BlockSpec((nj, rows, nk, lanes), lambda n: (0, n, 0, 0))
     sums, end = pl.pallas_call(
         functools.partial(sums_kernel, 1.0 / (nj * sizes[0])),
-        grid=(ni // rows,),
         out_shape=(jax.ShapeDtypeStruct(field_now.shape, f32),) * 2,
-        in_specs=[block, pl.BlockSpec((rows, nk, lanes), lambda n: (n, 0, 0))],
-        out_specs=[block, block],
+        in_specs=[pl.BlockSpec(memory_space=pltpu.VMEM)] * 2,
+        out_specs=[pl.BlockSpec(memory_space=pl.ANY)] * 2,
+        scratch_shapes=[pltpu.VMEM(field_now.shape, f32), dma((ni + 1,))],
+        compiler_params=pltpu.CompilerParams(vmem_limit_bytes=16 * 1024 * 1024),
         name="sums",
     )(end, below)
     return sums, end

time: 153 us -> 110 us (0.72)
  Pallas kernels: 149 us -> 108 us
  local copies, waits for them, and re-layouts: 2.72 us -> 0 us
    pallas_call x1, Pallas kernels: 142 us -> 104 us  [local(): pl.pallas_call(functools.partial(march_kernel, sizes), out_shape=(jax.Sha...]
    pallas_call x1, Pallas kernels: 7.32 us -> 3.41 us  [local(): pl.pallas_call(functools.partial(sums_kernel, 1.0 / (nj * sizes[0])), out...]
    unnamed x4 -> x0, local copies, waits for them, and re-layouts: 2.72 us -> none
where the time goes in v2:
time: 110 us; the launch traced here: 108 us
  Pallas kernels  108 us (98%)
    pallas_call x1, Pallas kernels, local(): pl.pallas_call(functools.partial(march_kernel, sizes), out_shape=(jax.Sha...  104 us
    pallas_call x1, Pallas kernels, local(): pl.pallas_call(functools.partial(sums_kernel, 1.0 / (nj * sizes[0])), out...  3.41 us

profile of v2, /device:TPU:8, one launch (start us, length us, event | category | flops | bytes accessed | tf_op | source)
XLA Modules:
  0.0 108.2 jit_solution(16894624428245843296)
XLA Ops:
  0.6 104.2 %march.1 = (f32[8,16,64,128]{3,2,1,0:T(8,128)S(1)}, f32[16,64,128]{2,1,0:T(8,128)S(1)}) custom-call(f32[8,16,64,128]{3,2,1,0:T(8,128)} %u_hbm.1, f32[8,16,64,128]{3,2,1,0:T(8,128)} %e_hbm.1, f32[8,16,64,128]{3,2,1,0:T(8,128)} %c_hbm.1), custom_call_target="tpu_custom_call" | custom-call | tf_op jit(solution)/shard_map/march/pallas_call | solution.py:328
  104.8 3.4 %sums.1 = (f32[8,16,64,128]{3,2,1,0:T(8,128)}, f32[8,16,64,128]{3,2,1,0:T(8,128)}) custom-call(f32[8,16,64,128]{3,2,1,0:T(8,128)S(1)} %get-tuple-element.4.field_ref, f32[16,64,128]{2,1,0:T(8,128)S(1)} %get-tuple-element.5.below_ref), custom_call_target="tpu_custom_call" | custom-call | tf_op jit(solution)/shard_map/sums/pallas_call | solution.py:361

commit v3 on v2

--- a/solution.py
+++ b/solution.py
@@ -11,7 +11,7 @@
 MESH = pl.DeviceIdType.MESH
 PAD = 8
 CHUNKS = 4
-ORDER = (0, 3, 1, 2)
+ORDER = (1, 2, 0, 3)
 JUP, JDOWN, IUP, IDOWN = SIDES = range(4)
 STRAIGHT, ROUND, BESIDE = PARTS = ((0, 5), (5, 6), (11, 5))
 
@@ -19,8 +19,8 @@
 def march_kernel(
     sizes, u_hbm, e_hbm, c_hbm, end_hbm, below_hbm,
     field, speed, k_out, k_in, total, gathered, prefix, passing,
-    load_sem, send_sem, recv_sem, k_send_sem, k_recv_sem, pass_send_sem, pass_recv_sem,
-    out_sem, own_sem, t_send_sem, t_recv_sem, p_send_sem, p_recv_sem,
+    load_sem, send_sem, recv_sem, i_recv_sem, k_send_sem, k_recv_sem, pass_send_sem, pass_recv_sem,
+    out_sem, t_send_sem, t_recv_sem, p_send_sem, p_recv_sem,
 ):
     ny, nx, nz = sizes
     nj, ni, nk, _ = u_hbm.shape
@@ -40,12 +40,15 @@
         cells = (slice(None), slice(None), inner(piece))
         source = (u_hbm, e_hbm, c_hbm)[which].at[cells]
         target = speed.at[cells] if which == 2 else field.at[(which, *block)]
-        return pltpu.make_async_copy(source, target, load_sem.at[which, piece])
+        return pltpu.make_async_copy(source, target, load_sem.at[which])
 
     run, half = ny // 2, ny // 4
     place = lax.rem(y, run)
     ends = {JUP: place == run - 1, JDOWN: place == 0}
-    away = {(JUP, ROUND): 1 - half, (JUP, BESIDE): -1, (JDOWN, ROUND): half - 1, (JDOWN, BESIDE): 1}
+    away = {(JUP, ROUND): 1 - half, (JUP, BESIDE): -half - 1, (JDOWN, ROUND): half - 1, (JDOWN, BESIDE): half + 1}
+
+    def loaded(which):
+        pltpu.make_async_copy(c_hbm, speed, load_sem.at[which]).wait()
 
     def face(step, piece, side, part=None, passed=False):
         slot = step % 2
@@ -62,18 +65,12 @@
         axis = "py" if along_j else "px"
         to = (up if high else down)[axis]
         source, target = field.at[here], field.at[there]
-        arrived = recv_sem.at[step, piece, side]
-        if step == 0:
-            rows = inner(piece)
-            if along_j:
-                source = u_hbm.at[nj - 1 if high else 0, pl.ds(first, count), rows]
-            else:
-                source = u_hbm.at[:, ni - 1 if high else 0, rows]
+        arrived = (recv_sem if along_j else i_recv_sem).at[step % 2, piece]
         if passed:
             to = y + away[side, part]
-            target, arrived = passing.at[step, piece, pl.ds(0, count)], pass_recv_sem.at[step, piece]
-        return pltpu.make_async_remote_copy(
-            src_ref=source, dst_ref=target, send_sem=send_sem.at[step, piece, side], recv_sem=arrived,
+            target, arrived = passing.at[step, piece, pl.ds(0, count)], pass_recv_sem.at[step % 2, piece]
+        return pltpu.make_async_remote_copy(
+            src_ref=source, dst_ref=target, send_sem=send_sem.at[step % 2, piece], recv_sem=arrived,
             device_id={axis: to}, device_id_type=MESH,
         )
 
@@ -84,12 +81,16 @@
         there = (step % 2, 0 if high else nj + 1, pl.ds(1 + first, count), padded(piece))
         return pltpu.make_async_remote_copy(
             src_ref=passing.at[step, piece, pl.ds(0, count)], dst_ref=field.at[there],
-            send_sem=pass_send_sem.at[step, piece], recv_sem=recv_sem.at[step, piece, side],
+            send_sem=pass_send_sem.at[step % 2, piece], recv_sem=recv_sem.at[step % 2, piece],
             device_id={"py": to}, device_id_type=MESH,
         )
 
-    def send_faces(step, piece):
-        for side in SIDES:
+    def columns(count, sem):
+        cells = speed.at[pl.ds(0, count // ni), :, inner(0)]
+        return pltpu.make_async_copy(cells, cells, sem)
+
+    def send_faces(step, piece, sides=SIDES):
+        for side in sides:
             if side not in ends:
                 face(step, piece, side).start()
                 continue
@@ -111,6 +112,8 @@
 
     def relay(step, piece):
         def act(side, part):
+            if step >= 2:
+                pass_on(step - 2, piece, side, part).wait_send()
             face(step, piece, side, part, passed=True).wait_recv()
             pass_on(step, piece, side, part).start()
 
@@ -119,11 +122,11 @@
     def k_face(step, high):
         return pltpu.make_async_remote_copy(
             src_ref=k_out.at[step % 2, high], dst_ref=k_in.at[step % 2, high],
-            send_sem=k_send_sem.at[step, high], recv_sem=k_recv_sem.at[step, high],
+            send_sem=k_send_sem.at[step % 2, high], recv_sem=k_recv_sem.at[step % 2, high],
             device_id={"pz": (up if high else down)["pz"]}, device_id_type=MESH,
         )
 
-    def send_k_face(step, high):
+    def gather_k_face(step, high):
         slot = step % 2
         row = PAD + (nk - 1 if high else 0)
 
@@ -133,7 +136,6 @@
             return 0
 
         lax.fori_loop(0, nj, gather, 0)
-        k_face(step, high).start()
 
     def take_k_face(step, high):
         slot = step % 2
@@ -172,14 +174,14 @@
 
     def end_copy(piece):
         return pltpu.make_async_copy(
-            field.at[STEPS % 2, pl.ds(1, nj), pl.ds(1, ni), padded(piece)], end_hbm.at[:, :, inner(piece)], out_sem.at[piece]
+            field.at[STEPS % 2, pl.ds(1, nj), pl.ds(1, ni), padded(piece)], end_hbm.at[:, :, inner(piece)], out_sem.at[0]
         )
 
     def total_copy(piece, away):
         to = lax.rem(y + away, ny)
         return pltpu.make_async_remote_copy(
             src_ref=total.at[to, inner(piece)], dst_ref=gathered.at[piece, y],
-            send_sem=t_send_sem.at[piece], recv_sem=t_recv_sem.at[piece],
+            send_sem=t_send_sem, recv_sem=t_recv_sem.at[piece],
             device_id={"py": to}, device_id_type=MESH,
         )
 
@@ -187,12 +189,12 @@
         to = lax.rem(y + away, ny)
         return pltpu.make_async_remote_copy(
             src_ref=prefix.at[piece, to], dst_ref=below_hbm.at[y, inner(piece)],
-            send_sem=p_send_sem.at[piece], recv_sem=p_recv_sem.at[piece],
+            send_sem=p_send_sem, recv_sem=p_recv_sem,
             device_id={"py": to}, device_id_type=MESH,
         )
 
     def own_prefix(piece):
-        return pltpu.make_async_copy(prefix.at[piece, y], below_hbm.at[y, inner(piece)], own_sem.at[piece])
+        return pltpu.make_async_copy(prefix.at[piece, y], below_hbm.at[y, inner(piece)], out_sem.at[1])
 
     def others(sem):
         return pltpu.make_async_copy(gathered.at[0, pl.ds(0, ny - 1)], gathered.at[0, pl.ds(0, ny - 1)], sem)
@@ -219,8 +221,6 @@
         to_all(prefix_copy, piece)
         own_prefix(piece).start()
 
-    for piece in ORDER:
-        load(0, piece).start()
     barrier = pltpu.get_barrier_semaphore()
 
     def greet(away, _):
@@ -231,63 +231,72 @@
         for near in (up, down):
             pl.semaphore_signal(barrier, inc=1, device_id={axis: near[axis]}, device_id_type=MESH)
     lax.fori_loop(1, ny, greet, 0)
+    for which in range(3):
+        for piece in ORDER:
+            load(which, piece).start()
+    loaded(0)
+    for high in (0, 1):
+        gather_k_face(0, high)
     pl.semaphore_wait(barrier, ny - 1 + 4)
 
-    for piece in ORDER:
-        send_faces(0, piece)
-    for piece in ORDER:
-        for which in (1, 2):
-            load(which, piece).start()
-    for piece in ORDER:
-        load(0, piece).wait()
-        if piece == 0:
-            send_k_face(0, 0)
-        if piece == CHUNKS - 1:
-            send_k_face(0, 1)
+    for high in (0, 1):
+        k_face(0, high).start()
+    for at, piece in enumerate(ORDER):
+        if at >= 2:
+            relay(0, ORDER[at - 2])
+        send_faces(0, piece, SIDES if at < 2 else (JUP, JDOWN))
 
     for step in range(STEPS):
         for at, piece in enumerate(ORDER):
-            if step == 0:
-                for which in (1, 2):
-                    load(which, piece).wait()
+            if step == 0 and at == 0:
+                loaded(1)
+                loaded(2)
             if piece == 0:
                 take_k_face(step, 1)
             if piece == CHUNKS - 1:
                 take_k_face(step, 0)
-            relay(step, piece)
-            for side in SIDES:
-                if step >= 1:
-                    face(step - 1, piece, side).wait_send()
-                face(step, piece, side).wait_recv()
+            if step >= 1:
+                relay(step, piece)
+            elif at in (1, 2):
+                relay(step, ORDER[at + 1])
+            if step == STEPS - 1 and at == CHUNKS - 1:
+                send_prefixes(ORDER[0])
+            if step >= 1:
+                columns(2 * (nj + ni), send_sem.at[(step - 1) % 2, piece]).wait()
+            if step == 0 and at == 0:
+                for n in (0, 1):
+                    columns(2 * nj, i_recv_sem.at[0, ORDER[n]]).wait()
+                    send_faces(0, ORDER[n + 2], (IUP, IDOWN))
+            elif step >= 1 or at >= 2:
+                columns(2 * nj, i_recv_sem.at[step % 2, piece]).wait()
+            columns(2 * ni, recv_sem.at[step % 2, piece]).wait()
             advance(step, piece)
             if step < STEPS - 1:
-                send_faces(step + 1, piece)
                 for high, owner in ((0, 0), (1, CHUNKS - 1)):
                     if piece == owner:
                         if step >= 1:
                             k_face(step - 1, high).wait_send()
-                        send_k_face(step + 1, high)
+                        gather_k_face(step + 1, high)
+                        k_face(step + 1, high).start()
+                send_faces(step + 1, piece)
             else:
                 end_copy(piece).start()
                 send_totals(piece)
-                if at >= 2:
-                    send_prefixes(ORDER[at - 2])
-    for piece in ORDER[2:]:
+    for piece in ORDER[1:]:
         send_prefixes(piece)
     for piece in ORDER:
-        for side in SIDES:
-            face(STEPS - 1, piece, side).wait_send()
-        end_copy(piece).wait()
-        own_prefix(piece).wait()
-        others(t_send_sem.at[piece]).wait()
-        others(p_send_sem.at[piece]).wait()
-        others(p_recv_sem.at[piece]).wait()
+        columns(2 * (nj + ni), send_sem.at[(STEPS - 1) % 2, piece]).wait()
+    pltpu.make_async_copy(speed, end_hbm, out_sem.at[0]).wait()
+    pltpu.make_async_copy(total.at[0], total.at[0], out_sem.at[1]).wait()
+    for sem in (t_send_sem, p_send_sem, p_recv_sem):
+        all_others = gathered.at[:, pl.ds(0, ny - 1)]
+        pltpu.make_async_copy(all_others, all_others, sem).wait()
     for step in (STEPS - 2, STEPS - 1):
         for high in (0, 1):
             k_face(step, high).wait_send()
 
     def passed_on(side, part):
-        for step in range(STEPS):
+        for step in (STEPS - 2, STEPS - 1):
             for piece in ORDER:
                 pass_on(step, piece, side, part).wait_send()
 
@@ -339,19 +348,19 @@
             pltpu.VMEM((CHUNKS, ni, kc, lanes), f32),
             pltpu.VMEM((CHUNKS, ni, kc, lanes), f32),
             pltpu.VMEM((STEPS, CHUNKS, max(ROUND[1], BESIDE[1]), kc, lanes), f32),
-            dma((3, CHUNKS)),
-            dma((STEPS, CHUNKS, len(SIDES))),
-            dma((STEPS, CHUNKS, len(SIDES))),
-            dma((STEPS, 2)),
-            dma((STEPS, 2)),
-            dma((STEPS, CHUNKS)),
-            dma((STEPS, CHUNKS)),
+            dma((3,)),
+            dma((2, CHUNKS)),
+            dma((2, CHUNKS)),
+            dma((2, CHUNKS)),
+            dma((2, 2)),
+            dma((2, 2)),
+            dma((2, CHUNKS)),
+            dma((2, CHUNKS)),
+            dma((2,)),
+            dma,
             dma((CHUNKS,)),
-            dma((CHUNKS,)),
-            dma((CHUNKS,)),
-            dma((CHUNKS,)),
-            dma((CHUNKS,)),
-            dma((CHUNKS,)),
+            dma,
+            dma,
         ],
         compiler_params=pltpu.CompilerParams(
             collective_id=0, has_side_effects=True, vmem_limit_bytes=48 * 1024 * 1024

time: 110 us -> 99 us (0.900)
  the two profiles are of different devices: /device:TPU:8 before, /device:TPU:224 now
where the time goes in v3:
time: 99 us; the launch traced here: 98.9 us
  Pallas kernels  98.3 us (99%)
    pallas_call x1, Pallas kernels, local(): pl.pallas_call(functools.partial(march_kernel, sizes), out_shape=(jax.Sha...  94.9 us
    pallas_call x1, Pallas kernels, local(): pl.pallas_call(functools.partial(sums_kernel, 1.0 / (nj * sizes[0])), out...  3.41 us

profile of v3, /device:TPU:224, one launch (start us, length us, event | category | flops | bytes accessed | tf_op | source)
XLA Modules:
  0.0 98.9 jit_solution(10165981127190976510)
XLA Ops:
  0.6 94.9 %march.1 = (f32[8,16,64,128]{3,2,1,0:T(8,128)S(1)}, f32[16,64,128]{2,1,0:T(8,128)S(1)}) custom-call(f32[8,16,64,128]{3,2,1,0:T(8,128)} %u_hbm.1, f32[8,16,64,128]{3,2,1,0:T(8,128)} %e_hbm.1, f32[8,16,64,128]{3,2,1,0:T(8,128)} %c_hbm.1), custom_call_target="tpu_custom_call" | custom-call | tf_op jit(solution)/shard_map/march/pallas_call | solution.py:337
  95.5 3.4 %sums.1 = (f32[8,16,64,128]{3,2,1,0:T(8,128)}, f32[8,16,64,128]{3,2,1,0:T(8,128)}) custom-call(f32[8,16,64,128]{3,2,1,0:T(8,128)S(1)} %get-tuple-element.4.field_ref, f32[16,64,128]{2,1,0:T(8,128)S(1)} %get-tuple-element.5.below_ref), custom_call_target="tpu_custom_call" | custom-call | tf_op jit(solution)/shard_map/sums/pallas_call | solution.py:370

commit v4 on v3

--- a/solution.py
+++ b/solution.py
@@ -13,7 +13,7 @@
 CHUNKS = 4
 ORDER = (1, 2, 0, 3)
 JUP, JDOWN, IUP, IDOWN = SIDES = range(4)
-STRAIGHT, ROUND, BESIDE = PARTS = ((0, 5), (5, 6), (11, 5))
+STRAIGHT, ROUND, BESIDE = PARTS = ((0, 7), (7, 5), (12, 4))
 
 
 def march_kernel(
@@ -89,6 +89,10 @@
         cells = speed.at[pl.ds(0, count // ni), :, inner(0)]
         return pltpu.make_async_copy(cells, cells, sem)
 
+    def send_parts(step, piece, side):
+        for part in (ROUND, BESIDE):
+            face(step, piece, side, part, passed=True).start()
+
     def send_faces(step, piece, sides=SIDES):
         for side in sides:
             if side not in ends:
@@ -97,8 +101,8 @@
 
             @pl.when(ends[side])
             def _():
-                for part in (ROUND, BESIDE):
-                    face(step, piece, side, part, passed=True).start()
+                if step >= 1:
+                    send_parts(step, piece, side)
                 face(step, piece, side, STRAIGHT).start()
 
             @pl.when(jnp.logical_not(ends[side]))
@@ -241,6 +245,13 @@
 
     for high in (0, 1):
         k_face(0, high).start()
+    for side, here in ends.items():
+
+        @pl.when(here)
+        def _():
+            for piece in ORDER:
+                send_parts(0, piece, side)
+
     for at, piece in enumerate(ORDER):
         if at >= 2:
             relay(0, ORDER[at - 2])

time: 99 us -> 97.4 us (0.984)
  the two profiles are of different devices: /device:TPU:224 before, /device:TPU:8 now
where the time goes in v4:
time: 97.4 us; the launch traced here: 97.3 us
  Pallas kernels  96.7 us (99%)
    pallas_call x1, Pallas kernels, local(): pl.pallas_call(functools.partial(march_kernel, sizes), out_shape=(jax.Sha...  93.3 us
    pallas_call x1, Pallas kernels, local(): pl.pallas_call(functools.partial(sums_kernel, 1.0 / (nj * sizes[0])), out...  3.41 us

profile of v4, /device:TPU:8, one launch (start us, length us, event | category | flops | bytes accessed | tf_op | source)
XLA Modules:
  0.0 97.3 jit_solution(3289461104585601693)
XLA Ops:
  0.6 93.3 %march.1 = (f32[8,16,64,128]{3,2,1,0:T(8,128)S(1)}, f32[16,64,128]{2,1,0:T(8,128)S(1)}) custom-call(f32[8,16,64,128]{3,2,1,0:T(8,128)} %u_hbm.1, f32[8,16,64,128]{3,2,1,0:T(8,128)} %e_hbm.1, f32[8,16,64,128]{3,2,1,0:T(8,128)} %c_hbm.1), custom_call_target="tpu_custom_call" | custom-call | tf_op jit(solution)/shard_map/march/pallas_call | solution.py:348
  93.9 3.4 %sums.1 = (f32[8,16,64,128]{3,2,1,0:T(8,128)}, f32[8,16,64,128]{3,2,1,0:T(8,128)}) custom-call(f32[8,16,64,128]{3,2,1,0:T(8,128)S(1)} %get-tuple-element.4.field_ref, f32[16,64,128]{2,1,0:T(8,128)S(1)} %get-tuple-element.5.below_ref), custom_call_target="tpu_custom_call" | custom-call | tf_op jit(solution)/shard_map/sums/pallas_call | solution.py:381
